TPU v7x, 16 devices: a 4x2x1 block of a 4x4x8 slice. The times are simulated.
16 devices in a mesh: dp: 2 (over y, z), tp: 8 (over x, core).
Axes of the slice: x: 4, y: 2, z: 1, core: 2. Of those that a mesh axis runs over, the one named last changes fastest.
The devices are a block of a 4x4x8 slice.
Arguments:
- tokens: bfloat16 [8, 2048, 2048], P('dp'), parts along dimension 0
- seq_lens: int32 [8], P('dp'), parts along dimension 0
- w_q: bfloat16 [2048, 2048], P(None, 'tp')
- w_k: bfloat16 [2048, 2048], P(None, 'tp')
- w_v: bfloat16 [2048, 2048], P(None, 'tp')
- w_o: bfloat16 [2048, 2048], P('tp')
- g_q: bfloat16 [2048], P('tp')
- g_k: bfloat16 [2048], P('tp')
- g_attn: bfloat16 [2048], replicated
- g_mlp: bfloat16 [2048], replicated
- w_gate: bfloat16 [2048, 8192], P(None, 'tp')
- w_up: bfloat16 [2048, 8192], P(None, 'tp')
- w_down: bfloat16 [8192, 2048], P('tp')
Outputs:
- output 1: bfloat16 [8, 2048, 2048], P('dp'), parts along dimension 0
- output 2: bfloat16 [8, 16, 2048, 128], P('dp', 'tp'), parts along dimension 0
- output 3: bfloat16 [8, 16, 2048, 128], P('dp', 'tp'), parts along dimension 0
There are 2 independent parts. A program takes and returns all parts, laid end to end along the dimension named above; an argument that names none is the same for every part.
All inputs are finite; a program needn't handle non-finite values.
Results may differ from a plain program's by a relative error of at most 0.0182036.
Values are sent between devices in bfloat16 or wider.
A program may use at most 768 MiB of HBM per device.

v0:
```python
import jax
import jax.numpy as jnp
from jax import lax
from jax.sharding import PartitionSpec as P

HEAD_DIM = 128
ROPE_BASE = 500000.0
NORM_EPS = 1e-6


def rope_tables(seq_len, head_dim):
    half_dim = head_dim // 2
    inv_freq = ROPE_BASE ** (-2.0 * jnp.arange(half_dim, dtype=jnp.float32) / head_dim)
    angles = jnp.arange(seq_len, dtype=jnp.float32)[:, None] * inv_freq[None, :]
    angles = jnp.concatenate([angles, angles], axis=-1)
    return jnp.cos(angles), jnp.sin(angles)


def apply_rope(vecs, cos_tab, sin_tab, head_axes):
    half_dim = vecs.shape[-1] // 2
    table_shape = (cos_tab.shape[0],) + (1,) * head_axes + (cos_tab.shape[1],)
    rotated = jnp.concatenate([-vecs[..., half_dim:], vecs[..., :half_dim]], axis=-1)
    return vecs * cos_tab.reshape(table_shape) + rotated * sin_tab.reshape(table_shape)


def rms_scale(vals):
    return lax.rsqrt(jnp.mean(vals * vals, axis=-1, keepdims=True) + NORM_EPS)


def post_norm(base, branch, gain):
    branch32 = branch.astype(jnp.float32)
    return (base.astype(jnp.float32) + branch32 * rms_scale(branch32) * gain.astype(jnp.float32)).astype(jnp.bfloat16)


def solution(mesh):
    tp_size = mesh.shape['tp']

    def local_layer(tokens, seq_lens, w_q, w_k, w_v, w_o, g_q, g_k, g_attn, g_mlp, w_gate, w_up, w_down):
        prompts, seq_len = tokens.shape[0], tokens.shape[1]
        kv_local = w_k.shape[1] // HEAD_DIM
        group_size = w_q.shape[1] // w_k.shape[1]
        q_raw = jnp.einsum('bsd,dn->bsn', tokens, w_q, preferred_element_type=jnp.float32)
        k_raw = jnp.einsum('bsd,dn->bsn', tokens, w_k, preferred_element_type=jnp.float32)
        v_new = jnp.einsum('bsd,dn->bsn', tokens, w_v, preferred_element_type=jnp.float32).astype(jnp.bfloat16)
        q_sumsq = lax.psum(jnp.sum(q_raw * q_raw, axis=-1, keepdims=True), 'tp')
        k_sumsq = lax.psum(jnp.sum(k_raw * k_raw, axis=-1, keepdims=True), 'tp')
        q_norm = q_raw * lax.rsqrt(q_sumsq / (w_q.shape[1] * tp_size) + NORM_EPS) * g_q.astype(jnp.float32)
        k_norm = k_raw * lax.rsqrt(k_sumsq / (w_k.shape[1] * tp_size) + NORM_EPS) * g_k.astype(jnp.float32)
        cos_tab, sin_tab = rope_tables(seq_len, HEAD_DIM)
        queries = apply_rope(q_norm.reshape(prompts, seq_len, kv_local, group_size, HEAD_DIM), cos_tab, sin_tab, 2).astype(jnp.bfloat16)
        keys_new = apply_rope(k_norm.reshape(prompts, seq_len, kv_local, HEAD_DIM), cos_tab, sin_tab, 1).astype(jnp.bfloat16)
        k_cache = jnp.transpose(keys_new, (0, 2, 1, 3))
        v_cache = jnp.transpose(v_new.reshape(prompts, seq_len, kv_local, HEAD_DIM), (0, 2, 1, 3))
        scores = jnp.einsum('bsgrd,bgtd->bgrst', queries, k_cache, preferred_element_type=jnp.float32) * HEAD_DIM ** -0.5
        positions = jnp.arange(seq_len)
        allowed = (positions[None, None, :] <= positions[None, :, None]) & (positions[None, None, :] < seq_lens[:, None, None])
        scores = jnp.where(allowed[:, None, None], scores, -1e30)
        attn_probs = jax.nn.softmax(scores, axis=-1).astype(jnp.bfloat16)
        attn_out = jnp.einsum('bgrst,bgtd->bsgrd', attn_probs, v_cache, preferred_element_type=jnp.float32).astype(jnp.bfloat16)
        attn_part = jnp.einsum('bsn,nd->bsd', attn_out.reshape(prompts, seq_len, -1), w_o, preferred_element_type=jnp.float32).astype(jnp.bfloat16)
        attn_proj = lax.psum(attn_part, 'tp')
        hidden = post_norm(tokens, attn_proj, g_attn)
        gate_pre = jnp.einsum('bsd,df->bsf', hidden, w_gate, preferred_element_type=jnp.float32)
        up_proj = jnp.einsum('bsd,df->bsf', hidden, w_up, preferred_element_type=jnp.float32)
        act_out = (jax.nn.silu(gate_pre) * up_proj).astype(jnp.bfloat16)
        mlp_part = jnp.einsum('bsf,fd->bsd', act_out, w_down, preferred_element_type=jnp.float32).astype(jnp.bfloat16)
        mlp_out = lax.psum(mlp_part, 'tp')
        out_hidden = post_norm(hidden, mlp_out, g_mlp)
        return out_hidden, k_cache, v_cache

    return jax.shard_map(local_layer, mesh=mesh, in_specs=(P('dp', None, None), P('dp'), P(None, 'tp'), P(None, 'tp'), P(None, 'tp'), P('tp', None), P('tp'), P('tp'), P(), P(), P(None, 'tp'), P(None, 'tp'), P('tp', None)), out_specs=(P('dp', None, None), P('dp', 'tp', None, None), P('dp', 'tp', None, None)), check_vma=False)
```

profile of v0, /device:TPU:113, one launch (start us, length us, event | category | flops | bytes accessed | tf_op | source)
XLA Modules:
  0.0 1262.1 jit_solution(12276696981276673453)
XLA Ops:
  7.3 18.1 %multiply_reduce_fusion = (f32[4,2048]{1,0:T(4,128)}, f32[4,2048,256]{1,2,0:T(8,128)}) fusion(bf16[4,2048,2048]{2,1,0:T(8,128)(2,1)} %param.13, bf16[2048,256]{1,0:T(8,128)(2,1)} %param.15), kind=kOutput, calls=%fused_computation.34 | convolution fusion | flops 8594120704 | bytes 43024384 | tf_op jit(solution)/shard_map/bsd,dn->bsn/dot_general | solution.py:42
  25.4 18.8 %multiply_reduce_fusion.1 = (f32[4,2048]{1,0:T(4,128)}, f32[4,2048,256]{1,2,0:T(8,128)}) fusion(bf16[4,2048,2048]{2,1,0:T(8,128)(2,1)} %param.13, bf16[2048,256]{1,0:T(8,128)(2,1)S(1)} %copy-done.6), kind=kOutput, calls=%fused_computation.36 | convolution fusion | flops 8594120704 | bytes 43024384 | tf_op jit(solution)/shard_map/bsd,dn->bsn/dot_general | solution.py:43
  46.9 17.0 %convolution_convert_fusion.2 = bf16[4,2048,256]{1,2,0:T(8,128)(2,1)} fusion(bf16[4,2048,2048]{2,1,0:T(8,128)(2,1)} %param.13, bf16[2048,256]{1,0:T(8,128)(2,1)S(1)} %copy-done.7), kind=kOutput, calls=%fused_computation.45 | convolution fusion | flops 8592031744 | bytes 38797312 | tf_op jit(solution)/shard_map/bsd,dn->bsn/dot_general | solution.py:44
  63.9 10.2 broadcast_and_fusion
  78.1 18.6 %all-reduce.9.cloned.1.call-done = (f32[4,2048,1]{1,0,2:T(4,128)}, f32[4,2048,1]{1,0,2:T(4,128)}) async-done(((f32[4,2048,1]{1,0,2:T(4,128)}, f32[4,2048,1]{1,0,2:T(4,128)}), (f32[4,2048,1]{1,0,2:T(4,128)}, f32[4,2048,1]{1,0,2:T(4,128)})) %all-reduce.9.cloned.1.call-update) | async-done | bytes 65552 | tf_op jit(solution)/shard_map/psum | solution.py:46
  97.6 8.5 multiply_multiply_fusion.1
  106.1 8.7 copy.19
  114.8 12.8 %slice_negate_fusion = (f32[4,2048,2,64]{3,1,2,0:T(8,128)}, f32[4,2048,2,64]{3,1,2,0:T(8,128)}) fusion(f32[4,2048,2,128]{3,1,2,0:T(8,128)} %copy.19), kind=kLoop, calls=%fused_computation.25 | loop fusion | flops 1048576 | bytes 16777216 | tf_op jit(solution)/shard_map/neg | solution.py:22
  146.3 7.2 negate_bitcast_fusion
  160.4 8.7 copy.23
  169.0 11.5 fusion.19
  180.5 63.4 %fusion.1 = (f32[4,2,2048]{2,1,0:T(2,128)S(1)}, f32[4,2,2048,2048]{3,2,1,0:T(8,128)}) fusion(pred[4,2048,2048]{1,2,0:T(8,128)(4,1)} %broadcast_and_fusion, bf16[4,2,2048,128]{3,2,1,0:T(8,128)(2,1)} %fusion.19, f32[4,2048,2,64]{3,1,2,0:T(8,128)} %bitcast.89, f32[4,2048,2,64]{3,1,2,0:T(8,128)} %negate_bitcast_fusion, f32[4,2048,2,128]{3,1,2,0:T(8,128)} %copy.23, ...), kind=kOutput, calls=%fused_computation.4 | convolution fusion | flops 8701067264 | bytes 174129152 | tf_op jit(solution)/shard_map/bsgrd,bgtd->bgrst/dot_general | solution.py:54
  244.0 46.2 %fusion = f32[4,2,2048]{2,1,0:T(2,128)S(1)} fusion(f32[4,2,2048,2048]{3,2,1,0:T(8,128)} %get-tuple-element.16, f32[4,2,2048]{2,1,0:T(2,128)S(1)} %get-tuple-element.15, pred[4,2048,2048]{1,2,0:T(8,128)(4,1)} %broadcast_and_fusion), kind=kLoop, calls=%fused_computation.3 | loop fusion | flops 134201344 | bytes 151126016 | tf_op jit(solution)/shard_map/reduce_sum | solution.py:58
  290.2 55.9 %fusion.27 = bf16[4,2,128,2048]{3,2,1,0:T(8,128)(2,1)} fusion(bf16[4,2,2048,128]{2,3,1,0:T(8,128)(2,1)} %bitcast.92, f32[4,2,2048]{2,1,0:T(2,128)S(1)} %fusion, f32[4,2,2048]{2,1,0:T(2,128)S(1)} %get-tuple-element.15, f32[4,2,2048,2048]{3,2,1,0:T(8,128)} %get-tuple-element.16, pred[4,2048,2048]{1,2,0:T(8,128)(4,1)} %broadcast_and_fusion), kind=kOutput, calls=%fused_computation.46 | convolution fusion | flops 8759803904 | bytes 159514624 | tf_op jit(solution)/shard_map/bgrst,bgtd->bsgrd/dot_general | solution.py:59
  346.1 16.7 %convolution_convert_fusion.1 = bf16[4,2048,2048]{2,1,0:T(8,128)(2,1)} fusion(bf16[4,2048,256]{1,2,0:T(8,128)(2,1)} %bitcast.91, bf16[256,2048]{1,0:T(8,128)(2,1)S(1)} %copy-done), kind=kOutput, calls=%fused_computation.22 | convolution fusion | flops 8606711808 | bytes 38797312 | tf_op jit(solution)/shard_map/bsn,nd->bsd/dot_general | solution.py:60
  363.5 332.3 %all-reduce.5.cloned.1.call-done = bf16[4,2048,2048]{2,1,0:T(8,128)(2,1)} async-done(((bf16[4,2048,2048]{2,1,0:T(8,128)(2,1)}), bf16[4,2048,2048]{2,1,0:T(8,128)(2,1)}) %all-reduce.5.cloned.1.call-update) | async-done | bytes 33554448 | tf_op jit(solution)/shard_map/psum | solution.py:61
  695.8 11.3 fusion.2
  707.2 33.4 %fusion.5 = bf16[4,2048,2048]{2,1,0:T(8,128)(2,1)} fusion(bf16[4,2048,2048]{2,1,0:T(8,128)(2,1)} %all-reduce.5.cloned.1.call-done, bf16[4,2048,2048]{2,1,0:T(8,128)(2,1)} %param.13, f32[2048]{0:T(1024)S(1)} %convert_element_type.75, f32[4,2048]{1,0:T(4,128)S(1)} %add_rsqrt_fusion.1), kind=kLoop, calls=%fused_computation.12 | loop fusion | flops 100663296 | bytes 100704256 | tf_op jit(solution)/shard_map/convert_element_type | solution.py:32
  740.6 42.4 %fusion.21 = f32[4,2048,1024]{2,1,0:T(8,128)} fusion(bf16[4,2048,2048]{2,1,0:T(8,128)(2,1)} %fusion.5, bf16[2048,1024]{1,0:T(8,128)(2,1)} %param.24), kind=kOutput, calls=%fused_computation.40 | convolution fusion | flops 34359738368 | bytes 71303168 | tf_op jit(solution)/shard_map/bsd,df->bsf/dot_general | solution.py:64
  783.0 49.9 %multiply_convert_fusion.clone.4 = bf16[4,2048,1024]{2,1,0:T(8,128)(2,1)} fusion(f32[4,2048,1024]{2,1,0:T(8,128)} %fusion.21, bf16[4,2048,2048]{2,1,0:T(8,128)(2,1)} %fusion.5, bf16[2048,1024]{1,0:T(8,128)(2,1)} %param.23), kind=kOutput, calls=%fused_computation.19.clone.clone.clone.1 | convolution fusion | flops 34410070016 | bytes 88080384 | tf_op jit(solution)/shard_map/bsd,df->bsf/dot_general | solution.py:63
  832.9 45.3 %convolution_convert_fusion = bf16[4,2048,2048]{2,1,0:T(8,128)(2,1)} fusion(bf16[1024,2048]{1,0:T(8,128)(2,1)} %param.25, bf16[4,2048,1024]{2,1,0:T(8,128)(2,1)} %multiply_convert_fusion.clone.4), kind=kOutput, calls=%fused_computation.21 | convolution fusion | flops 34376515584 | bytes 54525952 | tf_op jit(solution)/shard_map/bsf,fd->bsd/dot_general | solution.py:66
  885.1 325.1 %all-reduce.7.cloned.1.call-done = bf16[4,2048,2048]{2,1,0:T(8,128)(2,1)} async-done(((bf16[4,2048,2048]{2,1,0:T(8,128)(2,1)}), bf16[4,2048,2048]{2,1,0:T(8,128)(2,1)}) %all-reduce.7.cloned.1.call-update) | async-done | bytes 33554448 | tf_op jit(solution)/shard_map/psum | solution.py:67
  1210.2 11.3 fusion.6
  1221.5 33.5 %fusion.9 = bf16[4,2048,2048]{2,1,0:T(8,128)(2,1)} fusion(bf16[4,2048,2048]{2,1,0:T(8,128)(2,1)} %all-reduce.7.cloned.1.call-done, bf16[4,2048,2048]{2,1,0:T(8,128)(2,1)} %fusion.5, f32[2048]{0:T(1024)S(1)} %convert_element_type.81, f32[4,2048]{1,0:T(4,128)S(1)} %add_rsqrt_fusion), kind=kLoop, calls=%fused_computation.16 | loop fusion | flops 100663296 | bytes 100704256 | tf_op jit(solution)/shard_map/convert_element_type | solution.py:32
  (43 shorter events, 40.6 us)
Async XLA Ops:
  7.2 338.9 %copy-start = (bf16[256,2048]{1,0:T(8,128)(2,1)S(1)}, bf16[256,2048]{1,0:T(8,128)(2,1)}, u32[]{:S(2)}) copy-start(bf16[256,2048]{1,0:T(8,128)(2,1)} %param.18) | copy-start | bytes 3145732
  7.2 18.2 %copy-start.6 = (bf16[2048,256]{1,0:T(8,128)(2,1)S(1)}, bf16[2048,256]{1,0:T(8,128)(2,1)}, u32[]{:S(2)}) copy-start(bf16[2048,256]{1,0:T(8,128)(2,1)} %param.16) | copy-start | bytes 3145732
  7.2 89.6 %all-reduce.9.cloned.1.call-start = ((), (), s32[]{:S(2)}) async-start(), calls=%async_computation.2 | async-start | bytes 131072 | tf_op jit(solution)/shard_map/psum | solution.py:46
  25.4 21.4 %copy-start.5 = (s32[4]{0:T(128)S(1)}, s32[4]{0:T(128)}, u32[]{:S(2)}) copy-start(s32[4]{0:T(128)} %param.14) | copy-start | bytes 52
  25.4 21.5 %copy-start.7 = (bf16[2048,256]{1,0:T(8,128)(2,1)S(1)}, bf16[2048,256]{1,0:T(8,128)(2,1)}, u32[]{:S(2)}) copy-start(bf16[2048,256]{1,0:T(8,128)(2,1)} %param.17) | copy-start | bytes 3145732
  44.3 651.5 %all-reduce.5.cloned.1.call-start = ((), (), s32[]{:S(2)}) async-start(), calls=%async_computation | async-start | bytes 67108864 | tf_op jit(solution)/shard_map/psum | solution.py:61
  63.9 14.2 %copy-start.8 = (bf16[256]{0:T(256)(128)(2,1)S(1)}, bf16[256]{0:T(256)(128)(2,1)}, u32[]{:S(2)}) copy-start(bf16[256]{0:T(256)(128)(2,1)} %param.20) | copy-start | bytes 1540
  63.9 14.2 %copy-start.9 = (bf16[256]{0:T(256)(128)(2,1)S(1)}, bf16[256]{0:T(256)(128)(2,1)}, u32[]{:S(2)}) copy-start(bf16[256]{0:T(256)(128)(2,1)} %param.19) | copy-start | bytes 1540
  132.2 3.2 copy-start.2
  362.8 0.7 copy-start.3
  362.8 847.3 %all-reduce.7.cloned.1.call-start = ((), (), s32[]{:S(2)}) async-start(), calls=%async_computation.1 | async-start | bytes 67108864 | tf_op jit(solution)/shard_map/psum | solution.py:67
  878.2 0.7 copy-start.4
  1221.5 33.5 %copy-start.1 = (bf16[256,2048]{1,0:T(8,128)(2,1)S(1)}, bf16[256,2048]{1,0:T(8,128)(2,1)}, u32[]{:S(2)}) copy-start(bf16[256,2048]{1,0:T(8,128)(2,1)} %param.18) | copy-start | bytes 3145732
Sparse Core Ops, SparseCore 0:
  44.4 52.3 all-reduce.8
  362.9 332.7 all-reduce.4
  878.4 331.7 all-reduce.6
where the time goes:
time: 1270 us; the launch traced here: 1260 us
  waiting for transfers between devices  676 us (53%)
  matrix products  328 us (26%)
  other arithmetic  198 us (16%)
  local copies, waits for them, and re-layouts  45.7 us (4%)
  between operations  14.4 us (1%)
    psum x1, waiting for transfers between devices, local_layer(): attn_proj = lax.psum(attn_part, 'tp')  332 us
    psum x1, waiting for transfers between devices, local_layer(): mlp_out = lax.psum(mlp_part, 'tp')  325 us
    convert_element_type x2, other arithmetic, post_norm(): (base.astype(jnp.float32) + branch32 * rms_scale(branch32) * gain.astype(...  66.9 us
    dot_general x1, matrix products, local_layer(): jnp.einsum('bsgrd,bgtd->bgrst', queries, k_cache, preferred_element_type=...  63.4 us
    dot_general x1, matrix products, local_layer(): jnp.einsum('bgrst,bgtd->bsgrd', attn_probs, v_cache, preferred_element_ty...  55.9 us
    dot_general x1, matrix products, local_layer(): jnp.einsum('bsd,df->bsf', hidden, w_gate, preferred_element_type=jnp.floa...  49.9 us
    reduce_sum x1, other arithmetic, local_layer(): attn_probs = jax.nn.softmax(scores, axis=-1).astype(jnp.bfloat16)  46.2 us
    dot_general x1, matrix products, local_layer(): jnp.einsum('bsf,fd->bsd', act_out, w_down, preferred_element_type=jnp.flo...  45.3 us
  transfers between devices with their start and end apart: 3, of which 3 were waited for; matrix products, arithmetic and copies ran while one was open for 3% of the time, Pallas kernels for 0%

commit v1 on v0

v1 whole, which is shorter than its diff:
```python
import functools
import math

import jax
import jax.numpy as jnp
from jax import lax
from jax.experimental import pallas as pl
from jax.experimental.pallas import tpu as pltpu
from jax.sharding import PartitionSpec as P

HEAD_DIM = 128
ROPE_BASE = 500000.0
NORM_EPS = 1e-6
ROWS = 512
F32 = jnp.float32
BF16 = jnp.bfloat16
MESH = pl.DeviceIdType.MESH
VMEM_BYTES = 67_000_000


def rope_tables(seq_len, head_dim):
    half_dim = head_dim // 2
    inv_freq = ROPE_BASE ** (-2.0 * jnp.arange(half_dim, dtype=F32) / head_dim)
    angles = jnp.arange(seq_len, dtype=F32)[:, None] * inv_freq[None, :]
    sin = jnp.sin(angles)
    cos = jnp.cos(angles)
    return jnp.concatenate([cos, cos], axis=-1), jnp.concatenate([-sin, sin], axis=-1)


def send(src, dst, send_sem, recv_sem, peer):
    pltpu.make_async_remote_copy(src_ref=src, dst_ref=dst, send_sem=send_sem, recv_sem=recv_sem, device_id={'tp': peer}, device_id_type=MESH).start()


def wait_for(ref, sem):
    pltpu.make_async_copy(ref, ref, sem).wait()


def neighbours(tp_size):
    me = lax.axis_index('tp')
    chips = tp_size // 2
    chip, core = me // 2, me % 2
    right = ((chip + 1) % chips) * 2 + core
    left = ((chip + chips - 1) % chips) * 2 + core
    return me, chip, core, right, left, chip * 2 + 1 - core


def qkv_kernel(x_ref, wq_ref, wk_ref, wv_ref, q_ref, k_ref, v_ref, ss_ref):
    x = x_ref[...]
    q = jnp.dot(x, wq_ref[...], preferred_element_type=F32)
    k = jnp.dot(x, wk_ref[...], preferred_element_type=F32)
    v = jnp.dot(x, wv_ref[...], preferred_element_type=F32).astype(BF16)
    q_ref[...] = q
    k_ref[...] = k
    for h in range(v_ref.shape[1]):
        v_ref[0, h] = v[:, h * HEAD_DIM:(h + 1) * HEAD_DIM]
    qs = jnp.sum(q * q, axis=-1, keepdims=True)
    ks = jnp.sum(k * k, axis=-1, keepdims=True)
    lane = lax.broadcasted_iota(jnp.int32, (q.shape[0], 128), 1)
    t = jnp.transpose(jnp.where(lane < 64, qs, ks))
    ss_ref[0:1] = t[0:1]
    ss_ref[1:2] = t[64:65]


def qkv(x, w_q, w_k, w_v, prompts):
    total, d = x.shape
    n = w_q.shape[1]
    heads = n // HEAD_DIM
    seq = total // prompts
    per = seq // ROWS
    whole = lambda a: pl.BlockSpec(a.shape, lambda i: (0, 0))
    return pl.pallas_call(
        qkv_kernel,
        grid=(total // ROWS,),
        in_specs=[pl.BlockSpec((ROWS, d), lambda i: (i, 0)), whole(w_q), whole(w_k), whole(w_v)],
        out_specs=[
            pl.BlockSpec((ROWS, n), lambda i: (i, 0)),
            pl.BlockSpec((ROWS, n), lambda i: (i, 0)),
            pl.BlockSpec((1, heads, ROWS, HEAD_DIM), lambda i: (i // per, 0, i % per, 0)),
            pl.BlockSpec((2, ROWS), lambda i: (0, i)),
        ],
        out_shape=[
            jax.ShapeDtypeStruct((total, n), F32),
            jax.ShapeDtypeStruct((total, n), F32),
            jax.ShapeDtypeStruct((prompts, heads, seq, HEAD_DIM), BF16),
            jax.ShapeDtypeStruct((2, total), F32),
        ],
        cost_estimate=pl.CostEstimate(flops=2 * total * d * n * 3, bytes_accessed=2 * total * d + 10 * total * n, transcendentals=0),
        name="qkv",
    )(x, w_q, w_k, w_v)


PASS, PASS2, USE, SLOTS = 2, 3, 4, 8


def attn_kernel(lens_ref, q_ref, k_ref, v_ref, ss_ref, cos_ref, sin_ref, gq_ref, gk_ref, wo_ref, x_ref, ga_ref, h_ref, kc_ref,
                k_s, o_buf, ss_all, ss_send, ss_recv, got_l, got_r, half_l, half_r, got_s, sent, free_l, free_r, free_s,
                *, tp_size, chunks, blocks, width):
    s = pl.program_id(0)
    me, chip, core, right, left, sib = neighbours(tp_size)
    rows, n = q_ref.shape
    heads = kc_ref.shape[1]
    mid = rows // 2

    def cols(dev):
        return pl.ds(pl.multiple_of(dev * n, n), n)

    @pl.when(s == 0)
    def _():
        barrier = pltpu.get_barrier_semaphore()
        for d in range(1, tp_size):
            pl.semaphore_signal(barrier, inc=1, device_id={'tp': (me + d) % tp_size}, device_id_type=MESH)
        pl.semaphore_wait(barrier, tp_size - 1)
        for d in range(1, tp_size):
            send(ss_ref, ss_all.at[me], ss_send.at[d], ss_recv.at[me], (me + d) % tp_size)
        ss_all[pl.ds(me, 1)] = ss_ref[...][None]
        for d in range(1, tp_size):
            peer = (me + d) % tp_size
            wait_for(ss_all.at[peer], ss_recv.at[peer])
            wait_for(ss_ref, ss_send.at[d])

    @pl.when((s >= PASS) & (s < chunks + PASS))
    def _():
        slot = (s - PASS) % SLOTS
        buf = o_buf.at[slot]
        wait_for(buf.at[:, cols(left)], got_l.at[slot])
        first = buf.at[pl.ds(0, mid), cols(left)]
        send(first, first, sent.at[slot], half_l.at[slot], right)
        send(buf.at[:, cols(left)], buf.at[:, cols(left)], sent.at[slot], got_s.at[slot], sib)
        wait_for(buf.at[:, cols(right)], got_r.at[slot])
        second = buf.at[pl.ds(mid, mid), cols(right)]
        send(second, second, sent.at[slot], half_r.at[slot], left)
        send(buf.at[:, cols(right)], buf.at[:, cols(right)], sent.at[slot], got_s.at[slot], sib)

    @pl.when(s < chunks)
    def _():
        ss = jnp.sum(ss_all[:, :, pl.ds(pl.multiple_of(s * rows, rows), rows)], axis=0)
        scale = lax.rsqrt(ss / width + NORM_EPS)
        col_scale = jnp.transpose(jnp.concatenate([scale, jnp.zeros((6, rows), F32)], axis=0))
        cos, sin = cos_ref[...], sin_ref[...]

        def rope(t):
            return (t * cos + pltpu.roll(t, HEAD_DIM // 2, axis=1) * sin).astype(BF16)

        i = s % blocks
        b = s // blocks
        length = lens_ref[b]
        slot = s % SLOTS
        qn = q_ref[...] * col_scale[:, 0:1] * gq_ref[...]
        kn = k_ref[...] * col_scale[:, 1:2] * gk_ref[...]
        qh = []
        for h in range(heads):
            sl = slice(h * HEAD_DIM, (h + 1) * HEAD_DIM)
            kr = rope(kn[:, sl])
            kc_ref[0, h] = kr
            k_s[h, pl.ds(pl.multiple_of(i * rows, rows), rows), :] = kr
            qh.append(rope(qn[:, sl]))
        c = HEAD_DIM ** -0.5 * math.log2(math.e)
        for j in range(blocks):
            @pl.when(i == j)
            def _():
                kv = (j + 1) * rows
                col = lax.broadcasted_iota(jnp.int32, (1, kv), 1)
                bias = jnp.where(col < length, 0.0, -1e30).astype(F32)
                r = lax.broadcasted_iota(jnp.int32, (rows, rows), 0)
                cc = lax.broadcasted_iota(jnp.int32, (rows, rows), 1)
                tri = jnp.where(cc <= r, 0.0, -1e30).astype(F32)
                for h in range(heads):
                    sc = lax.dot_general(qh[h], k_s[h, 0:kv, :], (((1,), (1,)), ((), ())), preferred_element_type=F32)
                    sc = sc + bias
                    diag = sc[:, j * rows:] + tri
                    sc = diag if j == 0 else jnp.concatenate([sc[:, :j * rows], diag], axis=1)
                    m = jnp.max(sc, axis=-1, keepdims=True)
                    e = jnp.exp2(sc * c - m * c)
                    p = (e * (1.0 / jnp.sum(e, axis=-1, keepdims=True))).astype(BF16)
                    o = jnp.dot(p, v_ref[0, h, 0:kv, :], preferred_element_type=F32)
                    o_buf[slot, :, pl.ds(pl.multiple_of(me * n + h * HEAD_DIM, HEAD_DIM), HEAD_DIM)] = o.astype(BF16)

    @pl.when((s >= PASS2) & (s < chunks + PASS2))
    def _():
        slot = (s - PASS2) % SLOTS
        buf = o_buf.at[slot]
        far = ((chip + 2) % (tp_size // 2)) * 2 + core
        first = buf.at[pl.ds(0, mid), cols(far)]
        second = buf.at[pl.ds(mid, mid), cols(far)]
        wait_for(first, half_l.at[slot])
        send(first, first, sent.at[slot], got_s.at[slot], sib)
        wait_for(second, half_r.at[slot])
        send(second, second, sent.at[slot], got_s.at[slot], sib)

    @pl.when((s >= USE) & (s < chunks + USE))
    def _():
        t = s - USE
        slot = t % SLOTS
        buf = o_buf.at[slot]
        wait_for(buf.at[:, pl.ds(0, 4 * n)], got_s.at[slot])
        wait_for(buf.at[:, pl.ds(0, 7 * n)], sent.at[slot])
        d = h_ref.shape[1]
        step = 512
        sq = jnp.zeros((rows, 1), F32)
        for lo in range(0, d, step):
            a = jnp.dot(o_buf[slot], wo_ref[:, lo:lo + step], preferred_element_type=F32).astype(BF16)
            h_ref[:, lo:lo + step] = a
            a = a.astype(F32)
            sq = sq + jnp.sum(a * a, axis=-1, keepdims=True)
        scale = lax.rsqrt(sq / d + NORM_EPS)
        for lo in range(0, d, step):
            a = h_ref[:, lo:lo + step].astype(F32)
            h_ref[:, lo:lo + step] = (x_ref[:, lo:lo + step].astype(F32) + a * scale * ga_ref[:, lo:lo + step]).astype(BF16)

        @pl.when(t < chunks - SLOTS)
        def _():
            for sem, peer in ((free_r, left), (free_l, right), (free_s, sib)):
                pl.semaphore_signal(sem, inc=1, device_id={'tp': peer}, device_id_type=MESH)

    @pl.when(s < chunks)
    def _():
        slot = s % SLOTS

        @pl.when(s >= SLOTS)
        def _():
            for sem in (free_r, free_l, free_s):
                pl.semaphore_wait(sem, 1)

        own = o_buf.at[slot, :, cols(me)]
        send(own, own, sent.at[slot], got_l.at[slot], right)
        send(own, own, sent.at[slot], got_r.at[slot], left)
        send(own, own, sent.at[slot], got_s.at[slot], sib)


def attend(q, k, v, ss, cos, sin, g_q, g_k, lens, w_o, x, g_attn, tp_size):
    prompts, heads, seq, _ = v.shape
    n = heads * HEAD_DIM
    total, d = x.shape
    blocks = seq // ROWS
    chunks = total // ROWS
    now = lambda s: jnp.minimum(s, chunks - 1)
    used = lambda s: jnp.clip(s - USE, 0, chunks - 1)
    vmem = pl.BlockSpec(memory_space=pltpu.VMEM)
    dma = pltpu.SemaphoreType.DMA
    return pl.pallas_call(
        functools.partial(attn_kernel, tp_size=tp_size, chunks=chunks, blocks=blocks, width=n * tp_size),
        grid=(chunks + USE,),
        in_specs=[
            pl.BlockSpec(memory_space=pltpu.SMEM),
            pl.BlockSpec((ROWS, n), lambda s: (now(s), 0)),
            pl.BlockSpec((ROWS, n), lambda s: (now(s), 0)),
            pl.BlockSpec((1, heads, seq, HEAD_DIM), lambda s: (now(s) // blocks, 0, 0, 0)),
            vmem,
            pl.BlockSpec((ROWS, HEAD_DIM), lambda s: (now(s) % blocks, 0)),
            pl.BlockSpec((ROWS, HEAD_DIM), lambda s: (now(s) % blocks, 0)),
            vmem, vmem, vmem,
            pl.BlockSpec((ROWS, d), lambda s: (used(s), 0)),
            vmem,
        ],
        out_specs=[
            pl.BlockSpec((ROWS, d), lambda s: (used(s), 0)),
            pl.BlockSpec((1, heads, ROWS, HEAD_DIM), lambda s: (now(s) // blocks, 0, now(s) % blocks, 0)),
        ],
        out_shape=[
            jax.ShapeDtypeStruct((total, d), BF16),
            jax.ShapeDtypeStruct((prompts, heads, seq, HEAD_DIM), BF16),
        ],
        scratch_shapes=[
            pltpu.VMEM((heads, seq, HEAD_DIM), BF16),
            pltpu.VMEM((SLOTS, ROWS, n * tp_size), BF16),
            pltpu.VMEM((tp_size,) + ss.shape, F32),
            dma((tp_size,)), dma((tp_size,)),
            dma((SLOTS,)), dma((SLOTS,)), dma((SLOTS,)), dma((SLOTS,)), dma((SLOTS,)), dma((SLOTS,)),
            pltpu.SemaphoreType.REGULAR, pltpu.SemaphoreType.REGULAR, pltpu.SemaphoreType.REGULAR,
        ],
        compiler_params=pltpu.CompilerParams(collective_id=1, has_side_effects=True, vmem_limit_bytes=VMEM_BYTES),
        cost_estimate=pl.CostEstimate(flops=2 * total * d * n * tp_size, bytes_accessed=4 * total * d, transcendentals=0),
        name="attend",
    )(lens, q, k, v, ss, cos, sin, g_q, g_k, w_o, x, g_attn)


ADD, MERGE, FINAL, RELAY, RELAY2, DONE = 1, 3, 5, 7, 9, 10
SIB_SLOTS = 3


def mlp_kernel(h_ref, wg_ref, wu_ref, wd_ref, gm_ref, y_ref, act_s, m_s, c_s, r_sib, r1_l, r1_r, r2_l, r2_r, h_own, y_own,
               sib_send, sib_recv, s1_send, r1_lsem, r1_rsem, s2_send, r2_lsem, r2_rsem,
               y_send, y_loc, y_l, y_r, yh_l, yh_r, yf_send, yh_send, y_sib, free_s, *, tp_size, chunks):
    s = pl.program_id(0)
    me, chip, core, right, left, sib = neighbours(tp_size)
    chips = tp_size // 2
    rows, d = h_ref.shape
    half = rows // 2
    piece = half // chips
    sub = piece // 2
    opp = (chip + 2) % chips
    rchip = (chip + 1) % chips
    lchip = (chip + chips - 1) % chips
    own = pl.ds(pl.multiple_of(core * half, half), half)
    other = pl.ds(pl.multiple_of((1 - core) * half, half), half)

    def at(p, off=0, size=piece):
        return pl.ds(pl.multiple_of(p * piece + off, sub), size)

    def y_rows(t, c, p, off=0, size=piece):
        return y_ref.at[pl.ds(pl.multiple_of(t * rows + c * half + p * piece + off, sub), size)]

    def stage(lag):
        return pl.when((s >= lag) & (s < chunks + lag))

    @pl.when(s == 0)
    def _():
        barrier = pltpu.get_barrier_semaphore()
        for peer in (right, left, sib):
            pl.semaphore_signal(barrier, inc=1, device_id={'tp': peer}, device_id_type=MESH)
        pl.semaphore_wait(barrier, 3)

    @stage(0)
    def _():
        f = act_s.shape[1]
        h = h_ref[...]
        for lo in range(0, f, 512):
            gate = jnp.dot(h, wg_ref[:, lo:lo + 512], preferred_element_type=F32)
            up = jnp.dot(h, wu_ref[:, lo:lo + 512], preferred_element_type=F32)
            act_s[:, lo:lo + 512] = (jax.nn.silu(gate) * up).astype(BF16)
        act = act_s[...]
        for lo in range(0, d, 512):
            m_s[s % SIB_SLOTS, :, lo:lo + 512] = jnp.dot(act, wd_ref[:, lo:lo + 512], preferred_element_type=F32).astype(BF16)
        h_own[s % 8] = h_ref[pl.ds(pl.multiple_of(core * half + chip * piece, piece), piece), :]

    @stage(ADD)
    def _():
        t = s - ADD
        slot, ms = t % 8, t % SIB_SLOTS
        wait_for(r_sib.at[ms], sib_recv.at[ms])
        wait_for(m_s.at[ms, other], sib_send.at[ms])
        c_s[slot] = (m_s[ms, own, :].astype(F32) + r_sib[ms].astype(F32)).astype(BF16)

        @pl.when(t < chunks - SIB_SLOTS)
        def _():
            pl.semaphore_signal(free_s, inc=1, device_id={'tp': sib}, device_id_type=MESH)

    @stage(MERGE)
    def _():
        slot = (s - MERGE) % 8
        wait_for(r1_l.at[slot], r1_lsem.at[slot])
        c_s[slot, at(rchip, 0, sub), :] = (c_s[slot, at(rchip, 0, sub), :].astype(F32) + r1_l[slot].astype(F32)).astype(BF16)
        wait_for(r1_r.at[slot], r1_rsem.at[slot])
        c_s[slot, at(lchip, sub, sub), :] = (c_s[slot, at(lchip, sub, sub), :].astype(F32) + r1_r[slot].astype(F32)).astype(BF16)

    @stage(FINAL)
    def _():
        t = s - FINAL
        slot = t % 8
        wait_for(r2_l.at[slot], r2_lsem.at[slot])
        wait_for(r2_r.at[slot], r2_rsem.at[slot])
        wait_for(c_s.at[slot, pl.ds(0, piece)], s1_send.at[slot])
        wait_for(c_s.at[slot, pl.ds(0, 2 * piece)], s2_send.at[slot])
        m = c_s[slot, at(chip), :].astype(F32) + r2_l[slot].astype(F32) + r2_r[slot].astype(F32)
        m = m.astype(BF16).astype(F32)
        scale = lax.rsqrt(jnp.sum(m * m, axis=-1, keepdims=True) / d + NORM_EPS)
        y_own[slot] = (h_own[slot].astype(F32) + m * scale * gm_ref[...]).astype(BF16)

    @stage(RELAY)
    def _():
        t = s - RELAY
        slot = t % 8
        from_l, from_r = y_rows(t, core, lchip), y_rows(t, core, rchip)
        wait_for(from_l, y_l.at[slot])
        first = y_rows(t, core, lchip, 0, sub)
        send(first, first, yf_send.at[slot], yh_l.at[slot], right)
        send(from_l, from_l, yf_send.at[slot], y_sib.at[t], sib)
        wait_for(from_r, y_r.at[slot])
        second = y_rows(t, core, rchip, sub, sub)
        send(second, second, yf_send.at[slot], yh_r.at[slot], left)
        send(from_r, from_r, yf_send.at[slot], y_sib.at[t], sib)

    @stage(RELAY2)
    def _():
        t = s - RELAY2
        slot = t % 8
        first, second = y_rows(t, core, opp, 0, sub), y_rows(t, core, opp, sub, sub)
        wait_for(first, yh_l.at[slot])
        send(first, first, yh_send.at[slot], y_sib.at[t], sib)
        wait_for(second, yh_r.at[slot])
        send(second, second, yh_send.at[slot], y_sib.at[t], sib)

    @stage(DONE)
    def _():
        t = s - DONE
        slot = t % 8
        base = pl.multiple_of(t * rows, rows)
        wait_for(y_ref.at[pl.ds(base, piece)], y_loc.at[slot])
        wait_for(y_ref.at[pl.ds(base, 3 * piece)], y_send.at[slot])
        wait_for(y_ref.at[pl.ds(base, 3 * piece)], yf_send.at[slot])
        wait_for(y_ref.at[pl.ds(base, piece)], yh_send.at[slot])
        wait_for(y_ref.at[pl.ds(base, chips * piece)], y_sib.at[t])

    @stage(FINAL)
    def _():
        t = s - FINAL
        slot = t % 8
        dst = y_rows(t, core, chip)
        send(y_own.at[slot], dst, y_send.at[slot], y_l.at[slot], right)
        send(y_own.at[slot], dst, y_send.at[slot], y_r.at[slot], left)
        send(y_own.at[slot], dst, y_send.at[slot], y_sib.at[t], sib)
        pltpu.make_async_copy(y_own.at[slot], dst, y_loc.at[slot]).start()

    @stage(MERGE)
    def _():
        slot = (s - MERGE) % 8
        send(c_s.at[slot, at(rchip)], r2_l.at[slot], s2_send.at[slot], r2_lsem.at[slot], right)
        send(c_s.at[slot, at(lchip)], r2_r.at[slot], s2_send.at[slot], r2_rsem.at[slot], left)

    @stage(ADD)
    def _():
        slot = (s - ADD) % 8
        send(c_s.at[slot, at(opp, 0, sub)], r1_l.at[slot], s1_send.at[slot], r1_lsem.at[slot], right)
        send(c_s.at[slot, at(opp, sub, sub)], r1_r.at[slot], s1_send.at[slot], r1_rsem.at[slot], left)

    @stage(0)
    def _():
        @pl.when(s >= SIB_SLOTS)
        def _():
            pl.semaphore_wait(free_s, 1)

        ms = s % SIB_SLOTS
        send(m_s.at[ms, other], r_sib.at[ms], sib_send.at[ms], sib_recv.at[ms], sib)


def mlp(h, w_gate, w_up, w_down, g_mlp, tp_size):
    total, d = h.shape
    f = w_gate.shape[1]
    chunks = total // ROWS
    half = ROWS // 2
    piece = half // (tp_size // 2)
    sub = piece // 2
    vmem = pl.BlockSpec(memory_space=pltpu.VMEM)
    dma = pltpu.SemaphoreType.DMA
    return pl.pallas_call(
        functools.partial(mlp_kernel, tp_size=tp_size, chunks=chunks),
        grid=(chunks + DONE,),
        in_specs=[pl.BlockSpec((ROWS, d), lambda s: (jnp.minimum(s, chunks - 1), 0)), vmem, vmem, vmem, vmem],
        out_specs=pl.BlockSpec(memory_space=pl.ANY),
        out_shape=jax.ShapeDtypeStruct((total, d), BF16),
        scratch_shapes=[
            pltpu.VMEM((ROWS, f), BF16),
            pltpu.VMEM((SIB_SLOTS, ROWS, d), BF16),
            pltpu.VMEM((8, half, d), BF16),
            pltpu.VMEM((SIB_SLOTS, half, d), BF16),
            pltpu.VMEM((8, sub, d), BF16), pltpu.VMEM((8, sub, d), BF16),
            pltpu.VMEM((8, piece, d), BF16), pltpu.VMEM((8, piece, d), BF16),
            pltpu.VMEM((8, piece, d), BF16), pltpu.VMEM((8, piece, d), BF16),
            dma((SIB_SLOTS,)), dma((SIB_SLOTS,)),
            dma((8,)), dma((8,)), dma((8,)), dma((8,)), dma((8,)), dma((8,)),
            dma((8,)), dma((8,)), dma((8,)), dma((8,)), dma((8,)), dma((8,)), dma((8,)), dma((8,)),
            dma((chunks,)),
            pltpu.SemaphoreType.REGULAR,
        ],
        compiler_params=pltpu.CompilerParams(collective_id=2, has_side_effects=True, vmem_limit_bytes=VMEM_BYTES),
        cost_estimate=pl.CostEstimate(flops=6 * total * d * f, bytes_accessed=4 * total * d, transcendentals=0),
        name="mlp",
    )(h, w_gate, w_up, w_down, g_mlp)


def solution(mesh):
    tp_size = mesh.shape['tp']

    def local_layer(tokens, seq_lens, w_q, w_k, w_v, w_o, g_q, g_k, g_attn, g_mlp, w_gate, w_up, w_down):
        prompts, seq, d = tokens.shape
        x = tokens.reshape(prompts * seq, d)
        w_o_full = lax.all_gather(w_o, 'tp', axis=0, tiled=True)
        q, k, v_cache, ss = qkv(x, w_q, w_k, w_v, prompts)
        cos, sin = rope_tables(seq, HEAD_DIM)
        row = lambda g: g.astype(F32)[None]
        h, k_cache = attend(q, k, v_cache, ss, cos, sin, row(g_q), row(g_k), seq_lens, w_o_full, x, row(g_attn), tp_size)
        y = mlp(h, w_gate, w_up, w_down, row(g_mlp), tp_size)
        return y.reshape(prompts, seq, d), k_cache, v_cache

    return jax.shard_map(local_layer, mesh=mesh, in_specs=(P('dp', None, None), P('dp'), P(None, 'tp'), P(None, 'tp'), P(None, 'tp'), P('tp', None), P('tp'), P('tp'), P(), P(), P(None, 'tp'), P(None, 'tp'), P('tp', None)), out_specs=(P('dp', None, None), P('dp', 'tp', None, None), P('dp', 'tp', None, None)), check_vma=False)
```

time: 1270 us -> 581 us (0.46)
  waiting for transfers between devices: 676 us -> 4.45 us
  Pallas kernels: 0 us -> 524 us
  matrix products: 328 us -> 0 us
  other arithmetic: 198 us -> 10.8 us
  local copies, waits for them, and re-layouts: 45.7 us -> 27.4 us
    psum x3 -> x0, waiting for transfers between devices: 676 us -> none  [the longest x1 332 us: local_layer(): attn_proj = lax.psum(attn_part, 'tp')]
    pallas_call x0 -> x3, Pallas kernels: none -> 524 us  [the longest x1 305 us: mlp(): pl.pallas_call(functools.partial(mlp_kernel, tp_size=tp_size, chunks=chun...]
    dot_general x9 -> x0, matrix products: 328 us -> none  [the longest x1 63.4 us: local_layer(): jnp.einsum('bsgrd,bgtd->bgrst', queries, k_cache, preferred_element_type=...]
    reduce_sum x3 -> x0, other arithmetic: 68.9 us -> none  [the longest x1 46.2 us: local_layer(): attn_probs = jax.nn.softmax(scores, axis=-1).astype(jnp.bfloat16)]
    convert_element_type x6 -> x0, other arithmetic: 67 us -> none  [the longest x2 66.9 us: post_norm(): (base.astype(jnp.float32) + branch32 * rms_scale(branch32) * gain.astype(...]
    reshape x3 -> x0, local copies, waits for them, and re-layouts: 23.5 us -> none  [the longest x1 8.68 us: local_layer(): k_norm.reshape(prompts, seq_len, kv_local, HEAD_DIM)]
    mul x4 -> x0, other arithmetic: 14.2 us -> none  [the longest x1 8.54 us: local_layer(): k_raw * lax.rsqrt(k_sumsq / (w_k.shape[1] * tp_size) + NORM_EPS)]
    unnamed x22 -> x2, local copies, waits for them, and re-layouts: 18.2 us -> 27.4 us
  transfers between devices with their start and end apart: 3 -> 1, of which waited for: 3 -> 1; matrix products, arithmetic and copies ran while one was open for 3% -> 2% of each run, Pallas kernels for 0% -> 6%
where the time goes in v1:
time: 581 us
  Pallas kernels  524 us (90%)
  local copies, waits for them, and re-layouts  27.4 us (5%)
  between operations  14.1 us (2%)
  other arithmetic  10.8 us (2%)
    pallas_call x1, Pallas kernels, mlp(): pl.pallas_call(functools.partial(mlp_kernel, tp_size=tp_size, chunks=chun...  305 us
    pallas_call x1, Pallas kernels, attend(): pl.pallas_call(functools.partial(attn_kernel, tp_size=tp_size, chunks=chu...  183 us
    pallas_call x1, Pallas kernels, qkv(): pl.pallas_call(qkv_kernel, grid=(total // ROWS,), in_specs=[pl.BlockSpec(...  35.9 us
    unnamed x2, local copies, waits for them, and re-layouts  27.4 us
  transfers between devices with their start and end apart: 1, of which 1 were waited for; matrix products, arithmetic and copies ran while one was open for 2% of the time, Pallas kernels for 6%

profile of v1, /device:TPU:113, one launch (start us, length us, event | category | flops | bytes accessed | tf_op | source)
XLA Modules:
  0.0 580.6 jit_solution(4211969514448658434)
XLA Ops:
  7.2 0.1 all-gather.2.cloned.1.call-start
  7.2 0.7 all-gather.2.cloned.1.call-update
  8.0 1.2 broadcast_in_dim.30
  9.2 1.2 broadcast_in_dim.31
  10.4 1.3 broadcast_in_dim.32
  11.6 1.3 broadcast_in_dim.33
  12.9 3.9 fusion.2
  16.8 1.9 pad_maximum_fusion
  18.8 35.9 %qkv.1 = (f32[8192,256]{1,0:T(8,128)}, f32[8192,256]{1,0:T(8,128)}, bf16[4,2,2048,128]{3,2,1,0:T(8,128)(2,1)}, f32[2,8192]{1,0:T(2,128)}) custom-call(bf16[8192,2048]{1,0:T(8,128)(2,1)} %bitcast.9, bf16[2048,256]{1,0:T(8,128)(2,1)} %wq_ref.1, bf16[2048,256]{1,0:T(8,128)(2,1)} %wk_ref.1, bf16[2048,256]{1,0:T(8,128)(2,1)} %wv_ref.1), custom_call_target="tpu_custom_call" | custom-call | flops 25769803776 | bytes 54525952 | tf_op jit(solution)/shard_map/qkv/pallas_call | solution.py:71
  54.7 3.7 all-gather.2.cloned.1.call-done.wo_ref
  58.4 182.5 %attend.1 = (bf16[8192,2048]{1,0:T(8,128)(2,1)}, bf16[4,2,2048,128]{3,2,1,0:T(8,128)(2,1)}) custom-call(s32[4]{0:T(128)} %lens_ref.1, f32[8192,256]{1,0:T(8,128)} %get-tuple-element.9.q_ref, f32[8192,256]{1,0:T(8,128)} %get-tuple-element.10.k_ref, bf16[4,2,2048,128]{3,2,1,0:T(8,128)(2,1)} %get-tuple-element.25.v_ref, f32[2,8192]{1,0:T(2,128)} %get-tuple-element.12.ss_ref, ...), custom_call_target="tpu_custom_call" | custom-call | flops 68719476736 | bytes 67108864 | tf_op jit(solution)/shard_map/attend/pallas_call | solution.py:240
  240.9 305.4 %mlp.1 = bf16[8192,2048]{1,0:T(8,128)(2,1)} custom-call(bf16[8192,2048]{1,0:T(8,128)(2,1)} %get-tuple-element.13.h_ref, bf16[2048,1024]{1,0:T(8,128)(2,1)} %wg_ref.1, bf16[2048,1024]{1,0:T(8,128)(2,1)} %wu_ref.1, bf16[1024,2048]{1,0:T(8,128)(2,1)} %wd_ref.1, f32[1,2048]{1,0:T(1,128)} %bitcast.7), custom_call_target="tpu_custom_call" | custom-call | flops 103079215104 | bytes 67108864 | tf_op jit(solution)/shard_map/mlp/pallas_call | solution.py:435
  546.3 22.9 %copy.18 = bf16[4,2048,2048]{2,1,0:T(8,128)(2,1)} copy(bf16[4,2048,2048]{2,1,0:T(8,128)(2,1)} %bitcast.6) | data formatting | bytes 67108864
  569.2 4.5 copy.19
  (1 shorter events, 0.0 us)
Async XLA Ops:
  7.2 51.2 %all-gather.2.cloned.1.call-start = ((), (), s32[]{:S(2)}) async-start(), calls=%async_computation | async-start | bytes 9437184 | tf_op jit(solution)/shard_map/all_gather | solution.py:467
Sparse Core Ops, SparseCore 0:
  9.6 48.7 all-gather.1

commit v2 on v1

v2 whole, which is shorter than its diff:
```python
import functools
import math

import jax
import jax.numpy as jnp
import numpy as np
from jax import lax
from jax.experimental import pallas as pl
from jax.experimental.pallas import tpu as pltpu
from jax.sharding import PartitionSpec as P

HEAD_DIM = 128
ROPE_BASE = 500000.0
NORM_EPS = 1e-6
ROWS = 512
MLP_ROWS = 256
LATE = 4
F32 = jnp.float32
BF16 = jnp.bfloat16
MESH = pl.DeviceIdType.MESH
VMEM_BYTES = 67_000_000


def rope_tables(rows, blocks, head_dim):
    half = head_dim // 2
    inv_freq = np.tile(ROPE_BASE ** (-2.0 * np.arange(half) / head_dim), 2)
    fine = np.arange(rows)[:, None] * inv_freq[None]
    coarse = np.arange(blocks)[:, None] * rows * inv_freq[None]
    return [f(a).astype(np.float32) for a in (fine, coarse) for f in (np.cos, np.sin)]


def send(src, dst, send_sem, recv_sem, peer):
    pltpu.make_async_remote_copy(src_ref=src, dst_ref=dst, send_sem=send_sem, recv_sem=recv_sem, device_id={'tp': peer}, device_id_type=MESH).start()


def wait_for(ref, sem):
    pltpu.make_async_copy(ref, ref, sem).wait()


def neighbours(tp_size):
    me = lax.axis_index('tp')
    chips = tp_size // 2
    chip, core = me // 2, me % 2
    right = ((chip + 1) % chips) * 2 + core
    left = ((chip + chips - 1) % chips) * 2 + core
    return me, chip, core, right, left, chip * 2 + 1 - core


ATT, PASS, PASS2, DONE1 = 2, 4, 5, 6
SUM_SLOTS, QK_SLOTS, WO_PIECES, WO_PASS, WO_PASS2 = 4, 3, 4, 5, 8


def attn_kernel(lens_ref, x_ref, wq_ref, wk_ref, wv_ref, g_ref, fcos_ref, fsin_ref, ccos_ref, csin_ref, wo_ref,
                o_ref, o_late, wo_all, kc_ref, vc_ref,
                q_s, k_s, kr_s, v_s, o_own, ss_own, ss_all, ss_send, ss_recv, o_send, o_loc, got_l, got_r, half_l, half_r, got_s, late_loc,
                pass_send, pass2_send, wo_send, wo_loc, wo_l, wo_r, wo_hl, wo_hr, wo_s, *, tp_size, chunks, blocks, width):
    s = pl.program_id(0)
    me, chip, core, right, left, sib = neighbours(tp_size)
    far = ((chip + 2) % (tp_size // 2)) * 2 + core
    rows = x_ref.shape[0]
    n = wq_ref.shape[1]
    heads = kc_ref.shape[1]
    mid = rows // 2
    wo_rows = wo_ref.shape[0]
    gathered = chunks - LATE

    def o_at(t, dev, off=0, size=rows):
        return o_ref.at[pl.ds(pl.multiple_of(t * rows + off, mid), size), pl.ds(pl.multiple_of(dev * n, n), n)]

    def wo_at(dev, off=0, size=wo_rows):
        return wo_all.at[pl.ds(pl.multiple_of(dev * wo_rows + off, wo_rows // WO_PIECES), size)]

    def stage(lag, count=chunks):
        return pl.when((s >= lag) & (s < count + lag))

    @pl.when(s == 0)
    def _():
        barrier = pltpu.get_barrier_semaphore()
        for d in range(1, tp_size):
            pl.semaphore_signal(barrier, inc=1, device_id={'tp': (me + d) % tp_size}, device_id_type=MESH)
        pl.semaphore_wait(barrier, tp_size - 1)
        pltpu.make_async_copy(wo_ref, wo_at(me), wo_loc).start()

    @stage(PASS + LATE, gathered)
    def _():
        t = s - PASS - LATE
        slot = t % 8
        from_l, from_r = o_at(t, left), o_at(t, right)
        wait_for(from_l, got_l.at[slot])
        first = o_at(t, left, 0, mid)
        send(first, first, pass_send.at[slot], half_l.at[slot], right)
        send(from_l, from_l, pass_send.at[slot], got_s.at[slot], sib)
        wait_for(from_r, got_r.at[slot])
        second = o_at(t, right, mid, mid)
        send(second, second, pass_send.at[slot], half_r.at[slot], left)
        send(from_r, from_r, pass_send.at[slot], got_s.at[slot], sib)

    @stage(0)
    def _():
        x = x_ref[...]
        slot = s % QK_SLOTS
        b = (s // blocks) % 2
        here = pl.ds(pl.multiple_of((s % blocks) * rows, rows), rows)
        q = jnp.dot(x, wq_ref[...], preferred_element_type=F32)
        q_s[slot] = q
        k = jnp.dot(x, wk_ref[...], preferred_element_type=F32)
        k_s[slot] = k
        v = jnp.dot(x, wv_ref[...], preferred_element_type=F32).astype(BF16)
        for h in range(heads):
            vh = v[:, h * HEAD_DIM:(h + 1) * HEAD_DIM]
            vc_ref[0, h] = vh
            v_s[b, h, here, :] = vh
        qs = jnp.sum(q * q, axis=-1, keepdims=True)
        ks = jnp.sum(k * k, axis=-1, keepdims=True)
        lane = lax.broadcasted_iota(jnp.int32, (rows, 128), 1)
        t = jnp.transpose(jnp.where(lane < 64, qs, ks))
        ss_own[s % SUM_SLOTS] = jnp.concatenate([t[0:1], t[64:65]], axis=0)

    @stage(ATT)
    def _():
        t = s - ATT
        sslot = t % SUM_SLOTS
        for d in range(1, tp_size):
            peer = (me + d) % tp_size
            wait_for(ss_all.at[sslot, peer], ss_recv.at[sslot, peer])
        wait_for(ss_all.at[sslot, pl.ds(0, tp_size - 1)], ss_send.at[sslot])
        ss = ss_own[sslot]
        for d in range(1, tp_size):
            ss = ss + ss_all[sslot, (me + d) % tp_size]
        scale = lax.rsqrt(ss / width + NORM_EPS)
        col_scale = jnp.transpose(jnp.concatenate([scale, jnp.zeros((6, rows), F32)], axis=0))
        i = t % blocks
        b = t // blocks
        slot = t % 8
        lane = lax.broadcasted_iota(jnp.int32, (1, HEAD_DIM), 1)
        ccos, csin = ccos_ref[pl.ds(i, 1), :], csin_ref[pl.ds(i, 1), :]
        cos = fcos_ref[...] * ccos - fsin_ref[...] * csin
        sin = (fsin_ref[...] * ccos + fcos_ref[...] * csin) * jnp.where(lane < HEAD_DIM // 2, -1.0, 1.0)

        def rope(u):
            return (u * cos + pltpu.roll(u, HEAD_DIM // 2, axis=1) * sin).astype(BF16)

        length = lens_ref[b]
        qn = q_s[t % QK_SLOTS] * col_scale[:, 0:1] * g_ref[:, 0:n]
        kn = k_s[t % QK_SLOTS] * col_scale[:, 1:2] * g_ref[:, n:2 * n]
        qh = []
        for h in range(heads):
            sl = slice(h * HEAD_DIM, (h + 1) * HEAD_DIM)
            kr = rope(kn[:, sl])
            kc_ref[0, h] = kr
            kr_s[h, pl.ds(pl.multiple_of(i * rows, rows), rows), :] = kr
            qh.append(rope(qn[:, sl]))
        c = HEAD_DIM ** -0.5 * math.log2(math.e)
        for j in range(blocks):
            @pl.when(i == j)
            def _():
                kv = (j + 1) * rows
                col = lax.broadcasted_iota(jnp.int32, (1, kv), 1)
                bias = jnp.where(col < length, 0.0, -1e30).astype(F32)
                r = lax.broadcasted_iota(jnp.int32, (rows, rows), 0)
                cc = lax.broadcasted_iota(jnp.int32, (rows, rows), 1)
                tri = jnp.where(cc <= r, 0.0, -1e30).astype(F32)
                for h in range(heads):
                    sc = lax.dot_general(qh[h], kr_s[h, 0:kv, :], (((1,), (1,)), ((), ())), preferred_element_type=F32)
                    sc = sc + bias
                    diag = sc[:, j * rows:] + tri
                    sc = diag if j == 0 else jnp.concatenate([sc[:, :j * rows], diag], axis=1)
                    m = jnp.max(sc, axis=-1, keepdims=True)
                    e = jnp.exp2(sc * c - m * c)
                    p = (e * (1.0 / jnp.sum(e, axis=-1, keepdims=True))).astype(BF16)
                    o = jnp.dot(p, v_s[b % 2, h, 0:kv, :], preferred_element_type=F32)
                    o_own[slot, :, h * HEAD_DIM:(h + 1) * HEAD_DIM] = o.astype(BF16)

    @stage(PASS2 + LATE, gathered)
    def _():
        t = s - PASS2 - LATE
        slot = t % 8
        first, second = o_at(t, far, 0, mid), o_at(t, far, mid, mid)
        wait_for(first, half_l.at[slot])
        send(first, first, pass2_send.at[slot], got_s.at[slot], sib)
        wait_for(second, half_r.at[slot])
        send(second, second, pass2_send.at[slot], got_s.at[slot], sib)

    @stage(DONE1 + LATE, gathered)
    def _():
        t = s - DONE1 - LATE
        slot = t % 8
        part = o_ref.at[pl.ds(pl.multiple_of(t * rows, rows), rows)]
        wait_for(part.at[:, pl.ds(0, 3 * n)], o_send.at[slot])
        wait_for(part.at[:, pl.ds(0, n)], o_loc.at[slot])
        wait_for(part.at[:, pl.ds(0, 3 * n)], pass_send.at[slot])
        wait_for(part.at[:, pl.ds(0, n)], pass2_send.at[slot])
        wait_for(part.at[:, pl.ds(0, 4 * n)], got_s.at[slot])

    @stage(0)
    def _():
        slot = s % SUM_SLOTS
        for d in range(1, tp_size):
            send(ss_own.at[slot], ss_all.at[slot, me], ss_send.at[slot], ss_recv.at[slot, me], (me + d) % tp_size)

    @stage(ATT, LATE)
    def _():
        t = s - ATT
        pltpu.make_async_copy(o_own.at[t % 8], o_late.at[pl.ds(pl.multiple_of(t * rows, rows), rows)], late_loc.at[t]).start()

    @stage(DONE1, LATE)
    def _():
        t = s - DONE1
        wait_for(o_own.at[t % 8], late_loc.at[t])

    @stage(ATT + LATE, gathered)
    def _():
        t = s - ATT - LATE
        slot = t % 8
        own = o_own.at[(t + LATE) % 8]
        send(own, o_at(t, me), o_send.at[slot], got_l.at[slot], right)
        send(own, o_at(t, me), o_send.at[slot], got_r.at[slot], left)
        send(own, o_at(t, me), o_send.at[slot], got_s.at[slot], sib)
        pltpu.make_async_copy(own, o_at(t, me), o_loc.at[slot]).start()

    @pl.when(s < WO_PIECES)
    def _():
        size = wo_rows // WO_PIECES
        piece = wo_ref.at[pl.ds(pl.multiple_of(s * size, size), size)]
        send(piece, wo_at(me, s * size, size), wo_send, wo_l, right)
        send(piece, wo_at(me, s * size, size), wo_send, wo_r, left)
        send(piece, wo_at(me, s * size, size), wo_send, wo_s, sib)

    @pl.when(s == WO_PASS)
    def _():
        size = wo_rows // 2
        wait_for(wo_at(left), wo_l)
        send(wo_at(left, 0, size), wo_at(left, 0, size), wo_send, wo_hl, right)
        send(wo_at(left), wo_at(left), wo_send, wo_s, sib)
        wait_for(wo_at(right), wo_r)
        send(wo_at(right, size, size), wo_at(right, size, size), wo_send, wo_hr, left)
        send(wo_at(right), wo_at(right), wo_send, wo_s, sib)

    @pl.when(s == WO_PASS2)
    def _():
        size = wo_rows // 2
        wait_for(wo_at(far, 0, size), wo_hl)
        send(wo_at(far, 0, size), wo_at(far, 0, size), wo_send, wo_s, sib)
        wait_for(wo_at(far, size, size), wo_hr)
        send(wo_at(far, size, size), wo_at(far, size, size), wo_send, wo_s, sib)

    @pl.when(s == chunks + DONE1 - 1)
    def _():
        wait_for(wo_ref, wo_loc)
        wait_for(wo_all.at[pl.ds(0, 7 * wo_rows)], wo_send)
        wait_for(wo_all.at[pl.ds(0, 4 * wo_rows)], wo_s)


def attend(x, prompts, w_q, w_k, w_v, gains, lens, w_o, tp_size):
    total, d = x.shape
    n = w_q.shape[1]
    heads = n // HEAD_DIM
    seq = total // prompts
    blocks = seq // ROWS
    chunks = total // ROWS
    now = lambda s: jnp.minimum(s, chunks - 1)
    att = lambda s: jnp.clip(s - ATT, 0, chunks - 1)
    vmem = pl.BlockSpec(memory_space=pltpu.VMEM)
    hbm = pl.BlockSpec(memory_space=pl.ANY)
    dma = pltpu.SemaphoreType.DMA
    cache = jax.ShapeDtypeStruct((prompts, heads, seq, HEAD_DIM), BF16)
    tables = [jnp.asarray(t) for t in rope_tables(ROWS, blocks, HEAD_DIM)]
    return pl.pallas_call(
        functools.partial(attn_kernel, tp_size=tp_size, chunks=chunks, blocks=blocks, width=n * tp_size),
        grid=(chunks + DONE1,),
        in_specs=[
            pl.BlockSpec(memory_space=pltpu.SMEM),
            pl.BlockSpec((ROWS, d), lambda s: (now(s), 0)),
            vmem, vmem, vmem, vmem, vmem, vmem, vmem, vmem, hbm,
        ],
        out_specs=[
            hbm, hbm, hbm,
            pl.BlockSpec((1, heads, ROWS, HEAD_DIM), lambda s: (att(s) // blocks, 0, att(s) % blocks, 0)),
            pl.BlockSpec((1, heads, ROWS, HEAD_DIM), lambda s: (now(s) // blocks, 0, now(s) % blocks, 0)),
        ],
        out_shape=[
            jax.ShapeDtypeStruct((total - LATE * ROWS, n * tp_size), BF16),
            jax.ShapeDtypeStruct((LATE * ROWS, n), BF16),
            jax.ShapeDtypeStruct((w_o.shape[0] * tp_size, w_o.shape[1]), BF16),
            cache, cache,
        ],
        scratch_shapes=[
            pltpu.VMEM((QK_SLOTS, ROWS, n), F32),
            pltpu.VMEM((QK_SLOTS, ROWS, n), F32),
            pltpu.VMEM((heads, seq, HEAD_DIM), BF16),
            pltpu.VMEM((2, heads, seq, HEAD_DIM), BF16),
            pltpu.VMEM((8, ROWS, n), BF16),
            pltpu.VMEM((SUM_SLOTS, 2, ROWS), F32),
            pltpu.VMEM((SUM_SLOTS, tp_size, 2, ROWS), F32),
            dma((SUM_SLOTS,)), dma((SUM_SLOTS, tp_size)),
            dma((8,)), dma((8,)), dma((8,)), dma((8,)), dma((8,)), dma((8,)), dma((8,)), dma((LATE,)), dma((8,)), dma((8,)),
            dma, dma, dma, dma, dma, dma, dma,
        ],
        compiler_params=pltpu.CompilerParams(collective_id=1, has_side_effects=True, vmem_limit_bytes=VMEM_BYTES),
        cost_estimate=pl.CostEstimate(flops=6 * total * d * n, bytes_accessed=4 * total * d, transcendentals=0),
        name="attend",
    )(lens, x, w_q, w_k, w_v, gains, *tables, w_o)


ADD, MERGE, FINAL, RELAY, RELAY2, DONE = 1, 3, 5, 7, 9, 10
LATE_PASS, LATE_PASS2, LATE_DONE = 4, 7, 14
SIB_SLOTS, C_SLOTS = 3, 6


def mlp_kernel(o_ref, late_ref, x_ref, wo_ref, g_ref, wg_ref, wu_ref, wd_ref, y_ref, o_late, o_s, h_ref, act_s, m_s, c_s, r_sib, r1_l, r1_r, r2_l, r2_r, h_own, y_own,
               sib_send, sib_recv, s1_send, r1_lsem, r1_rsem, s2_send, r2_lsem, r2_rsem,
               y_send, y_loc, y_l, y_r, yh_l, yh_r, yf_send, yh_send, y_sib, free_s, late_send, late_loc, late_l, late_r, late_hl, late_hr, late_s, *, tp_size, chunks, early):
    s = pl.program_id(0)
    me, chip, core, right, left, sib = neighbours(tp_size)
    chips = tp_size // 2
    rows, d = x_ref.shape
    n, late_mid = late_ref.shape[1], late_ref.shape[0] // 2
    g_at = g_ref.shape[1] - 2 * d
    half = rows // 2
    piece = half // chips
    sub = piece // 2
    opp = (chip + 2) % chips
    rchip = (chip + 1) % chips
    lchip = (chip + chips - 1) % chips
    own = pl.ds(pl.multiple_of(core * half, half), half)
    other = pl.ds(pl.multiple_of((1 - core) * half, half), half)

    def at(p, off=0, size=piece):
        return pl.ds(pl.multiple_of(p * piece + off, sub), size)

    def y_rows(t, c, p, off=0, size=piece):
        return y_ref.at[pl.ds(pl.multiple_of((t + chunks - early) % chunks * rows + c * half + p * piece + off, sub), size)]

    def late(dev, off=0, size=2 * late_mid):
        return o_late.at[pl.ds(off, size), pl.ds(pl.multiple_of(dev * n, n), n)]

    def stage(lag):
        return pl.when((s >= lag) & (s < chunks + lag))

    @pl.when(s == 0)
    def _():
        barrier = pltpu.get_barrier_semaphore()
        for peer in (right, left, sib):
            pl.semaphore_signal(barrier, inc=1, device_id={'tp': peer}, device_id_type=MESH)
        pl.semaphore_wait(barrier, 3)
        for peer, sem in ((right, late_l), (left, late_r), (sib, late_s)):
            send(late_ref, late(me), late_send, sem, peer)
        pltpu.make_async_copy(late_ref, late(me), late_loc).start()

    @pl.when(s == LATE_PASS)
    def _():
        wait_for(late(left), late_l)
        send(late(left, 0, late_mid), late(left, 0, late_mid), late_send, late_hl, right)
        send(late(left), late(left), late_send, late_s, sib)
        wait_for(late(right), late_r)
        send(late(right, late_mid, late_mid), late(right, late_mid, late_mid), late_send, late_hr, left)
        send(late(right), late(right), late_send, late_s, sib)

    @pl.when(s == LATE_PASS2)
    def _():
        far = opp * 2 + core
        wait_for(late(far, 0, late_mid), late_hl)
        send(late(far, 0, late_mid), late(far, 0, late_mid), late_send, late_s, sib)
        wait_for(late(far, late_mid, late_mid), late_hr)
        send(late(far, late_mid, late_mid), late(far, late_mid, late_mid), late_send, late_s, sib)

    @pl.when(s == LATE_DONE)
    def _():
        wait_for(late_ref, late_loc)
        wait_for(o_late.at[:, pl.ds(0, 7 * n)], late_send)
        wait_for(o_late.at[:, pl.ds(0, 4 * n)], late_s)

    @pl.when(s < early)
    def _():
        o_s[...] = o_ref[...]

    @pl.when((s >= early) & (s < chunks))
    def _():
        o_s[...] = o_late[pl.ds(pl.multiple_of((s - early) * rows, rows), rows), :]

    @stage(0)
    def _():
        f = act_s.shape[1]
        o = o_s[...]
        sq = jnp.zeros((rows, 1), F32)
        for lo in range(0, d, 512):
            a = jnp.dot(o, wo_ref[:, lo:lo + 512], preferred_element_type=F32).astype(BF16)
            h_ref[:, lo:lo + 512] = a
            a = a.astype(F32)
            sq = sq + jnp.sum(a * a, axis=-1, keepdims=True)
        scale = lax.rsqrt(sq / d + NORM_EPS)
        for lo in range(0, d, 512):
            a = h_ref[:, lo:lo + 512].astype(F32)
            h_ref[:, lo:lo + 512] = (x_ref[:, lo:lo + 512].astype(F32) + a * scale * g_ref[:, g_at + lo:g_at + lo + 512]).astype(BF16)
        h = h_ref[...]
        for lo in range(0, f, 512):
            gate = jnp.dot(h, wg_ref[:, lo:lo + 512], preferred_element_type=F32)
            up = jnp.dot(h, wu_ref[:, lo:lo + 512], preferred_element_type=F32)
            act_s[:, lo:lo + 512] = (jax.nn.silu(gate) * up).astype(BF16)
        act = act_s[...]
        for lo in range(0, d, 512):
            m_s[s % SIB_SLOTS, :, lo:lo + 512] = jnp.dot(act, wd_ref[:, lo:lo + 512], preferred_element_type=F32).astype(BF16)
        h_own[s % 8] = h_ref[pl.ds(pl.multiple_of(core * half + chip * piece, piece), piece), :]

    @stage(ADD)
    def _():
        t = s - ADD
        slot, ms, cs = t % 8, t % SIB_SLOTS, t % C_SLOTS
        wait_for(r_sib.at[ms], sib_recv.at[ms])
        wait_for(m_s.at[ms, other], sib_send.at[ms])
        c_s[cs] = (m_s[ms, own, :].astype(F32) + r_sib[ms].astype(F32)).astype(BF16)

        @pl.when(t < chunks - SIB_SLOTS)
        def _():
            pl.semaphore_signal(free_s, inc=1, device_id={'tp': sib}, device_id_type=MESH)

    @stage(MERGE)
    def _():
        slot, cs = (s - MERGE) % 8, (s - MERGE) % C_SLOTS
        wait_for(r1_l.at[slot], r1_lsem.at[slot])
        c_s[cs, at(rchip, 0, sub), :] = (c_s[cs, at(rchip, 0, sub), :].astype(F32) + r1_l[slot].astype(F32)).astype(BF16)
        wait_for(r1_r.at[slot], r1_rsem.at[slot])
        c_s[cs, at(lchip, sub, sub), :] = (c_s[cs, at(lchip, sub, sub), :].astype(F32) + r1_r[slot].astype(F32)).astype(BF16)

    @stage(FINAL)
    def _():
        t = s - FINAL
        slot, cs = t % 8, t % C_SLOTS
        wait_for(r2_l.at[slot], r2_lsem.at[slot])
        wait_for(r2_r.at[slot], r2_rsem.at[slot])
        wait_for(c_s.at[cs, pl.ds(0, piece)], s1_send.at[slot])
        wait_for(c_s.at[cs, pl.ds(0, 2 * piece)], s2_send.at[slot])
        m = c_s[cs, at(chip), :].astype(F32) + r2_l[slot].astype(F32) + r2_r[slot].astype(F32)
        m = m.astype(BF16).astype(F32)
        scale = lax.rsqrt(jnp.sum(m * m, axis=-1, keepdims=True) / d + NORM_EPS)
        y_own[slot] = (h_own[slot].astype(F32) + m * scale * g_ref[:, g_at + d:]).astype(BF16)

    @stage(RELAY)
    def _():
        t = s - RELAY
        slot = t % 8
        from_l, from_r = y_rows(t, core, lchip), y_rows(t, core, rchip)
        wait_for(from_l, y_l.at[slot])
        first = y_rows(t, core, lchip, 0, sub)
        send(first, first, yf_send.at[slot], yh_l.at[slot], right)
        send(from_l, from_l, yf_send.at[slot], y_sib.at[t], sib)
        wait_for(from_r, y_r.at[slot])
        second = y_rows(t, core, rchip, sub, sub)
        send(second, second, yf_send.at[slot], yh_r.at[slot], left)
        send(from_r, from_r, yf_send.at[slot], y_sib.at[t], sib)

    @stage(RELAY2)
    def _():
        t = s - RELAY2
        slot = t % 8
        first, second = y_rows(t, core, opp, 0, sub), y_rows(t, core, opp, sub, sub)
        wait_for(first, yh_l.at[slot])
        send(first, first, yh_send.at[slot], y_sib.at[t], sib)
        wait_for(second, yh_r.at[slot])
        send(second, second, yh_send.at[slot], y_sib.at[t], sib)

    @stage(DONE)
    def _():
        t = s - DONE
        slot = t % 8
        base = pl.multiple_of(t * rows, rows)
        wait_for(y_ref.at[pl.ds(base, piece)], y_loc.at[slot])
        wait_for(y_ref.at[pl.ds(base, 3 * piece)], y_send.at[slot])
        wait_for(y_ref.at[pl.ds(base, 3 * piece)], yf_send.at[slot])
        wait_for(y_ref.at[pl.ds(base, piece)], yh_send.at[slot])
        wait_for(y_ref.at[pl.ds(base, chips * piece)], y_sib.at[t])

    @stage(FINAL)
    def _():
        t = s - FINAL
        slot = t % 8
        dst = y_rows(t, core, chip)
        send(y_own.at[slot], dst, y_send.at[slot], y_l.at[slot], right)
        send(y_own.at[slot], dst, y_send.at[slot], y_r.at[slot], left)
        send(y_own.at[slot], dst, y_send.at[slot], y_sib.at[t], sib)
        pltpu.make_async_copy(y_own.at[slot], dst, y_loc.at[slot]).start()

    @stage(MERGE)
    def _():
        slot, cs = (s - MERGE) % 8, (s - MERGE) % C_SLOTS
        send(c_s.at[cs, at(rchip)], r2_l.at[slot], s2_send.at[slot], r2_lsem.at[slot], right)
        send(c_s.at[cs, at(lchip)], r2_r.at[slot], s2_send.at[slot], r2_rsem.at[slot], left)

    @stage(ADD)
    def _():
        slot, cs = (s - ADD) % 8, (s - ADD) % C_SLOTS
        send(c_s.at[cs, at(opp, 0, sub)], r1_l.at[slot], s1_send.at[slot], r1_lsem.at[slot], right)
        send(c_s.at[cs, at(opp, sub, sub)], r1_r.at[slot], s1_send.at[slot], r1_rsem.at[slot], left)

    @stage(0)
    def _():
        @pl.when(s >= SIB_SLOTS)
        def _():
            pl.semaphore_wait(free_s, 1)

        ms = s % SIB_SLOTS
        send(m_s.at[ms, other], r_sib.at[ms], sib_send.at[ms], sib_recv.at[ms], sib)


def mlp(o, late, x, w_o, gains, w_gate, w_up, w_down, tp_size):
    total, d = x.shape
    f = w_gate.shape[1]
    chunks = total // MLP_ROWS
    half = MLP_ROWS // 2
    piece = half // (tp_size // 2)
    sub = piece // 2
    early = o.shape[0] // MLP_ROWS
    front = pl.BlockSpec((MLP_ROWS, d), lambda s: (jnp.minimum(s, early - 1), 0))
    chunk = pl.BlockSpec((MLP_ROWS, d), lambda s: ((jnp.minimum(s, chunks - 1) + chunks - early) % chunks, 0))
    vmem = pl.BlockSpec(memory_space=pltpu.VMEM)
    dma = pltpu.SemaphoreType.DMA
    return pl.pallas_call(
        functools.partial(mlp_kernel, tp_size=tp_size, chunks=chunks, early=early),
        grid=(chunks + DONE,),
        in_specs=[front, pl.BlockSpec(memory_space=pl.ANY), chunk, vmem, vmem, vmem, vmem, vmem],
        out_specs=pl.BlockSpec(memory_space=pl.ANY),
        out_shape=jax.ShapeDtypeStruct((total, d), BF16),
        scratch_shapes=[
            pltpu.VMEM((late.shape[0], d), BF16),
            pltpu.VMEM((MLP_ROWS, d), BF16),
            pltpu.VMEM((MLP_ROWS, d), BF16),
            pltpu.VMEM((MLP_ROWS, f), BF16),
            pltpu.VMEM((SIB_SLOTS, MLP_ROWS, d), BF16),
            pltpu.VMEM((C_SLOTS, half, d), BF16),
            pltpu.VMEM((SIB_SLOTS, half, d), BF16),
            pltpu.VMEM((8, sub, d), BF16), pltpu.VMEM((8, sub, d), BF16),
            pltpu.VMEM((8, piece, d), BF16), pltpu.VMEM((8, piece, d), BF16),
            pltpu.VMEM((8, piece, d), BF16), pltpu.VMEM((8, piece, d), BF16),
            dma((SIB_SLOTS,)), dma((SIB_SLOTS,)),
            dma((8,)), dma((8,)), dma((8,)), dma((8,)), dma((8,)), dma((8,)),
            dma((8,)), dma((8,)), dma((8,)), dma((8,)), dma((8,)), dma((8,)), dma((8,)), dma((8,)),
            dma((chunks,)),
            pltpu.SemaphoreType.REGULAR,
            dma, dma, dma, dma, dma, dma, dma,
        ],
        compiler_params=pltpu.CompilerParams(collective_id=2, has_side_effects=True, vmem_limit_bytes=VMEM_BYTES),
        cost_estimate=pl.CostEstimate(flops=6 * total * d * f + 2 * total * d * d, bytes_accessed=4 * total * d, transcendentals=0),
        name="mlp",
    )(o, late, x, w_o, gains, w_gate, w_up, w_down)


def solution(mesh):
    tp_size = mesh.shape['tp']

    def local_layer(tokens, seq_lens, w_q, w_k, w_v, w_o, g_q, g_k, g_attn, g_mlp, w_gate, w_up, w_down):
        prompts, seq, d = tokens.shape
        x = tokens.reshape(prompts * seq, d)
        gains = jnp.concatenate([g_q, g_k, g_attn, g_mlp]).astype(F32)[None]
        o, o_late, w_o_full, k_cache, v_cache = attend(x, prompts, w_q, w_k, w_v, gains, seq_lens, w_o, tp_size)
        y = mlp(o, o_late, x, w_o_full, gains, w_gate, w_up, w_down, tp_size)
        return y.reshape(prompts, seq, d), k_cache, v_cache

    return jax.shard_map(local_layer, mesh=mesh, in_specs=(P('dp', None, None), P('dp'), P(None, 'tp'), P(None, 'tp'), P(None, 'tp'), P('tp', None), P('tp'), P('tp'), P(), P(), P(None, 'tp'), P(None, 'tp'), P('tp', None)), out_specs=(P('dp', None, None), P('dp', 'tp', None, None), P('dp', 'tp', None, None)), check_vma=False)
```

time: 581 us -> 512 us (0.88)
  Pallas kernels: 524 us -> 478 us
  between operations: 14.1 us -> 0.65 us
  other arithmetic: 10.8 us -> 0.63 us
    pallas_call x1 -> x0, Pallas kernels: 35.9 us -> none  [qkv(): pl.pallas_call(qkv_kernel, grid=(total // ROWS,), in_specs=[pl.BlockSpec(...]
    pallas_call x1, Pallas kernels: 183 us -> 159 us  [attend(): pl.pallas_call(functools.partial(attn_kernel, tp_size=tp_size, chunks=chu...]
    pallas_call x1, Pallas kernels: 305 us -> 320 us  [mlp(): pl.pallas_call(functools.partial(mlp_kernel, tp_size=tp_size, chunks=chun...]
    unnamed x2 -> x5, local copies, waits for them, and re-layouts: 27.4 us -> 29.6 us
  transfers between devices with their start and end apart: 1 -> 0, of which waited for: 1 -> 0; matrix products, arithmetic and copies ran while one was open for 2% -> 0% of each run, Pallas kernels for 6% -> 0%
where the time goes in v2:
time: 512 us
  Pallas kernels  478 us (93%)
  local copies, waits for them, and re-layouts  32.3 us (6%)
    pallas_call x1, Pallas kernels, mlp(): pl.pallas_call(functools.partial(mlp_kernel, tp_size=tp_size, chunks=chun...  320 us
    pallas_call x1, Pallas kernels, attend(): pl.pallas_call(functools.partial(attn_kernel, tp_size=tp_size, chunks=chu...  159 us
    unnamed x5, local copies, waits for them, and re-layouts  29.6 us

profile of v2, /device:TPU:113, one launch (start us, length us, event | category | flops | bytes accessed | tf_op | source)
XLA Modules:
  0.0 511.9 jit_solution(4773646160724524163)
XLA Ops:
  0.6 0.7 concatenate.18
  1.3 0.7 concatenate.19
  1.9 0.7 concatenate.20
  2.6 0.7 concatenate.21
  3.3 0.6 maximum_convert_fusion.g_ref
  4.0 158.7 %attend.1 = (bf16[6144,2048]{1,0:T(8,128)(2,1)}, bf16[2048,256]{1,0:T(8,128)(2,1)}, bf16[2048,2048]{1,0:T(8,128)(2,1)}, bf16[4,2,2048,128]{3,2,1,0:T(8,128)(2,1)}, bf16[4,2,2048,128]{3,2,1,0:T(8,128)(2,1)}) custom-call(s32[4]{0:T(128)} %lens_ref.1, bf16[8192,2048]{1,0:T(8,128)(2,1)} %bitcast.3, bf16[2048,256]{1,0:T(8,128)(2,1)} %wq_ref.1, ...), custom_call_target="tpu_custom_call" | custom-call | flops 25769803776 | bytes 67108864 | tf_op jit(solution)/shard_map/attend/pallas_call | solution.py:268
  162.6 319.7 %mlp.1 = bf16[8192,2048]{1,0:T(8,128)(2,1)} custom-call(bf16[6144,2048]{1,0:T(8,128)(2,1)} %get-tuple-element.8.o_ref, bf16[2048,256]{1,0:T(8,128)(2,1)} %get-tuple-element.9.late_ref, bf16[8192,2048]{1,0:T(8,128)(2,1)} %bitcast.4, bf16[2048,2048]{1,0:T(8,128)(2,1)} %get-tuple-element.10.wo_ref, f32[1,4608]{1,0:T(1,128)} %maximum_convert_fusion.g_ref, ...), custom_call_target="tpu_custom_call" | custom-call | flops 171798691840 | bytes 67108864 | tf_op jit(solution)/shard_map/mlp/pallas_call | solution.py:517
  482.3 22.9 %copy.23 = bf16[4,2048,2048]{2,1,0:T(8,128)(2,1)} copy(bf16[4,2048,2048]{2,1,0:T(8,128)(2,1)} %bitcast.2) | data formatting | bytes 67108864
  505.2 0.0 copy-start
  505.2 4.7 copy.24
  509.9 0.0 copy-done
  509.9 2.0 copy.25
Async XLA Ops:
  505.2 4.7 copy-start

commit v3 on v2

--- a/solution.py
+++ b/solution.py
@@ -14,7 +14,7 @@
 NORM_EPS = 1e-6
 ROWS = 512
 MLP_ROWS = 256
-LATE = 4
+LATE = 5
 F32 = jnp.float32
 BF16 = jnp.bfloat16
 MESH = pl.DeviceIdType.MESH
@@ -69,6 +69,12 @@
 
     def wo_at(dev, off=0, size=wo_rows):
         return wo_all.at[pl.ds(pl.multiple_of(dev * wo_rows + off, wo_rows // WO_PIECES), size)]
+
+    def send_wo(i):
+        size = wo_rows // WO_PIECES
+        piece = wo_ref.at[pl.ds(pl.multiple_of(i * size, size), size)]
+        for peer, sem in ((right, wo_l), (left, wo_r), (sib, wo_s)):
+            send(piece, wo_at(me, i * size, size), wo_send, sem, peer)
 
     def stage(lag, count=chunks):
         return pl.when((s >= lag) & (s < count + lag))
@@ -220,11 +226,7 @@
 
     @pl.when(s < WO_PIECES)
     def _():
-        size = wo_rows // WO_PIECES
-        piece = wo_ref.at[pl.ds(pl.multiple_of(s * size, size), size)]
-        send(piece, wo_at(me, s * size, size), wo_send, wo_l, right)
-        send(piece, wo_at(me, s * size, size), wo_send, wo_r, left)
-        send(piece, wo_at(me, s * size, size), wo_send, wo_s, sib)
+        send_wo(s)
 
     @pl.when(s == WO_PASS)
     def _():
@@ -303,13 +305,13 @@
 
 
 ADD, MERGE, FINAL, RELAY, RELAY2, DONE = 1, 3, 5, 7, 9, 10
-LATE_PASS, LATE_PASS2, LATE_DONE = 4, 7, 14
+LATE_PASS, LATE_PASS2, LATE_DONE = 3, 5, 14
 SIB_SLOTS, C_SLOTS = 3, 6
 
 
-def mlp_kernel(o_ref, late_ref, x_ref, wo_ref, g_ref, wg_ref, wu_ref, wd_ref, y_ref, o_late, o_s, h_ref, act_s, m_s, c_s, r_sib, r1_l, r1_r, r2_l, r2_r, h_own, y_own,
+def mlp_kernel(o_ref, late_ref, x_ref, wo_in, g_ref, wg_in, wu_in, wd_in, y_ref, wo_ref, wg_ref, wu_ref, wd_ref, o_late, o_s, h_ref, act_s, m_s, c_s, r_sib, r1_l, r1_r, r2_l, r2_r, h_own, y_own,
                sib_send, sib_recv, s1_send, r1_lsem, r1_rsem, s2_send, r2_lsem, r2_rsem,
-               y_send, y_loc, y_l, y_r, yh_l, yh_r, yf_send, yh_send, y_sib, free_s, late_send, late_loc, late_l, late_r, late_hl, late_hr, late_s, *, tp_size, chunks, early):
+               y_send, y_loc, y_l, y_r, yh_l, yh_r, yf_send, yh_send, y_sib, free_s, late_send, late_loc, late_l, late_r, late_hl, late_hr, late_s, w_sem, *, tp_size, chunks, early):
     s = pl.program_id(0)
     me, chip, core, right, left, sib = neighbours(tp_size)
     chips = tp_size // 2
@@ -339,6 +341,10 @@
 
     @pl.when(s == 0)
     def _():
+        loads = [pltpu.make_async_copy(src, dst, w_sem.at[i]) for i, (src, dst) in enumerate(
+            ((wo_in, wo_ref), (wg_in, wg_ref), (wu_in, wu_ref), (wd_in, wd_ref)))]
+        for load in loads:
+            load.start()
         barrier = pltpu.get_barrier_semaphore()
         for peer in (right, left, sib):
             pl.semaphore_signal(barrier, inc=1, device_id={'tp': peer}, device_id_type=MESH)
@@ -346,6 +352,8 @@
         for peer, sem in ((right, late_l), (left, late_r), (sib, late_s)):
             send(late_ref, late(me), late_send, sem, peer)
         pltpu.make_async_copy(late_ref, late(me), late_loc).start()
+        for load in loads:
+            load.wait()
 
     @pl.when(s == LATE_PASS)
     def _():
@@ -513,14 +521,16 @@
     front = pl.BlockSpec((MLP_ROWS, d), lambda s: (jnp.minimum(s, early - 1), 0))
     chunk = pl.BlockSpec((MLP_ROWS, d), lambda s: ((jnp.minimum(s, chunks - 1) + chunks - early) % chunks, 0))
     vmem = pl.BlockSpec(memory_space=pltpu.VMEM)
+    hbm = pl.BlockSpec(memory_space=pl.ANY)
     dma = pltpu.SemaphoreType.DMA
     return pl.pallas_call(
         functools.partial(mlp_kernel, tp_size=tp_size, chunks=chunks, early=early),
         grid=(chunks + DONE,),
-        in_specs=[front, pl.BlockSpec(memory_space=pl.ANY), chunk, vmem, vmem, vmem, vmem, vmem],
-        out_specs=pl.BlockSpec(memory_space=pl.ANY),
+        in_specs=[front, hbm, chunk, hbm, vmem, hbm, hbm, hbm],
+        out_specs=hbm,
         out_shape=jax.ShapeDtypeStruct((total, d), BF16),
         scratch_shapes=[
+            pltpu.VMEM(w_o.shape, BF16), pltpu.VMEM(w_gate.shape, BF16), pltpu.VMEM(w_up.shape, BF16), pltpu.VMEM(w_down.shape, BF16),
             pltpu.VMEM((late.shape[0], d), BF16),
             pltpu.VMEM((MLP_ROWS, d), BF16),
             pltpu.VMEM((MLP_ROWS, d), BF16),
@@ -536,7 +546,7 @@
             dma((8,)), dma((8,)), dma((8,)), dma((8,)), dma((8,)), dma((8,)), dma((8,)), dma((8,)),
             dma((chunks,)),
             pltpu.SemaphoreType.REGULAR,
-            dma, dma, dma, dma, dma, dma, dma,
+            dma, dma, dma, dma, dma, dma, dma, dma((4,)),
         ],
         compiler_params=pltpu.CompilerParams(collective_id=2, has_side_effects=True, vmem_limit_bytes=VMEM_BYTES),
         cost_estimate=pl.CostEstimate(flops=6 * total * d * f + 2 * total * d * d, bytes_accessed=4 * total * d, transcendentals=0),

time: 512 us -> 506 us (0.988)
    pallas_call x1, Pallas kernels: 159 us -> 152 us  [attend(): pl.pallas_call(functools.partial(attn_kernel, tp_size=tp_size, chunks=chu...]
where the time goes in v3:
time: 506 us
  Pallas kernels  473 us (93%)
  local copies, waits for them, and re-layouts  32.3 us (6%)
    pallas_call x1, Pallas kernels, mlp(): pl.pallas_call(functools.partial(mlp_kernel, tp_size=tp_size, chunks=chun...  321 us
    pallas_call x1, Pallas kernels, attend(): pl.pallas_call(functools.partial(attn_kernel, tp_size=tp_size, chunks=chu...  152 us
    unnamed x5, local copies, waits for them, and re-layouts  29.6 us

profile of v3, /device:TPU:113, one launch (start us, length us, event | category | flops | bytes accessed | tf_op | source)
XLA Modules:
  0.0 506.2 jit_solution(6310542710574511360)
XLA Ops:
  0.6 0.7 concatenate.18
  1.3 0.7 concatenate.19
  1.9 0.7 concatenate.20
  2.6 0.7 concatenate.21
  3.3 0.6 maximum_convert_fusion.g_ref
  4.0 151.5 %attend.1 = (bf16[5632,2048]{1,0:T(8,128)(2,1)}, bf16[2560,256]{1,0:T(8,128)(2,1)}, bf16[2048,2048]{1,0:T(8,128)(2,1)}, bf16[4,2,2048,128]{3,2,1,0:T(8,128)(2,1)}, bf16[4,2,2048,128]{3,2,1,0:T(8,128)(2,1)}) custom-call(s32[4]{0:T(128)} %lens_ref.1, bf16[8192,2048]{1,0:T(8,128)(2,1)} %bitcast.3, bf16[2048,256]{1,0:T(8,128)(2,1)} %wq_ref.1, ...), custom_call_target="tpu_custom_call" | custom-call | flops 25769803776 | bytes 67108864 | tf_op jit(solution)/shard_map/attend/pallas_call | solution.py:270
  155.5 321.1 %mlp.1 = bf16[8192,2048]{1,0:T(8,128)(2,1)} custom-call(bf16[5632,2048]{1,0:T(8,128)(2,1)} %get-tuple-element.8.o_ref, bf16[2560,256]{1,0:T(8,128)(2,1)} %get-tuple-element.9.late_ref, bf16[8192,2048]{1,0:T(8,128)(2,1)} %bitcast.4, bf16[2048,2048]{1,0:T(8,128)(2,1)} %get-tuple-element.10.wo_in, f32[1,4608]{1,0:T(1,128)} %maximum_convert_fusion.g_ref, ...), custom_call_target="tpu_custom_call" | custom-call | flops 171798691840 | bytes 67108864 | tf_op jit(solution)/shard_map/mlp/pallas_call | solution.py:526
  476.6 22.9 %copy.23 = bf16[4,2048,2048]{2,1,0:T(8,128)(2,1)} copy(bf16[4,2048,2048]{2,1,0:T(8,128)(2,1)} %bitcast.2) | data formatting | bytes 67108864
  499.5 0.0 copy-start
  499.5 4.7 copy.24
  504.2 0.0 copy-done
  504.2 2.0 copy.25
Async XLA Ops:
  499.5 4.7 copy-start
